TPU v7x, 32 devices: a whole 2x2x4 slice. The times are simulated.
32 devices in a mesh: py: 2 (over x), px: 4 (over z), pz: 4 (over y, core).
Axes of the slice: x: 2, y: 2, z: 4, core: 2. Of those that a mesh axis runs over, the one named last changes fastest.
Arguments:
- field_now: float32 [16, 64, 256, 128], P('py', 'px', 'pz'), may hold values from 0.2 to 1.8
- earlier: float32 [16, 64, 256, 128], P('py', 'px', 'pz'), may hold values from 0.2 to 1.8
- speed_square: float32 [16, 64, 256, 128], P('py', 'px', 'pz'), may hold values from 0.05 to 0.3
Outputs:
- column_sum: float32 [16, 64, 256, 128], P('py', 'px', 'pz')
- field_now_end: float32 [16, 64, 256, 128], P('py', 'px', 'pz')
All inputs are finite; a program needn't handle non-finite values.
Results may differ from a plain program's by a relative error of at most 0.00002.
Values sent between devices are 32-bit elements; how exact they have to be, the bound alone decides.
A program may use at most 128 MiB of HBM per device.

v0:
```python
import jax
import jax.numpy as jnp
from jax import lax
from jax.sharding import PartitionSpec as P

STEPS = 4


def with_halo(value, sides, width):
    for axis, dim in sides:
        peers, length = (lax.axis_size(axis), value.shape[dim])
        up = [(i, (i + 1) % peers) for i in range(peers)]
        down = [(j, i) for i, j in up]
        last = lax.slice_in_dim(value, length - width, length, axis=dim)
        initial = lax.slice_in_dim(value, 0, width, axis=dim)
        before = lax.ppermute(last, axis, up)
        after = lax.ppermute(initial, axis, down)
        value = jnp.concatenate([before, value, after], axis=dim)
    return value


def prefix(value, axis, combine, identity):
    peers, mine = (lax.axis_size(axis), lax.axis_index(axis))
    everything = lax.all_gather(value, axis)
    start = jnp.broadcast_to(jnp.asarray(identity, value.dtype), value.shape)

    def hop(k, before):
        reached = k < mine
        new = combine(before, everything[k])
        return jnp.where(reached, new, before)

    return lax.fori_loop(0, peers, hop, start)


def without_rim(values, dims):
    for dim in dims:
        values = lax.slice_in_dim(values, 1, values.shape[dim] - 1, axis=dim)
    return values


def shifted_cells(values, dim, start, dims):
    others = [other for other in dims if other != dim]
    values = without_rim(values, others)
    return lax.slice_in_dim(values, start, start + values.shape[dim] - 2, axis=dim)


def march_step(padded, before, speed_square):
    middle = without_rim(padded, (0, 1, 2))
    lower = [shifted_cells(padded, dim, 0, (0, 1, 2)) for dim in (0, 1, 2)]
    upper = [shifted_cells(padded, dim, 2, (0, 1, 2)) for dim in (0, 1, 2)]
    spread = lower[0] + upper[0] + lower[1] + upper[1] + lower[2] + upper[2] - 6.0 * middle
    return 2.0 * middle - before + speed_square * spread


def local(field_now, earlier, speed_square):
    for step in range(STEPS):
        padded = with_halo(field_now, (("py", 0), ("px", 1), ("pz", 2)), 1)
        later = march_step(padded, earlier, speed_square)
        earlier, field_now = (field_now, later)
    here = jnp.cumsum(field_now, axis=0)
    total = lax.slice_in_dim(here, here.shape[0] - 1, here.shape[0], axis=0)

    def add_pair(earlier_total, later_total):
        return earlier_total + later_total

    below = prefix(total, "py", add_pair, jnp.zeros_like(total))
    column_sum = (here + below) / (field_now.shape[0] * lax.axis_size("py"))
    return (column_sum, field_now)


def solution(mesh):
    placed = (P("py", "px", "pz", None), P("py", "px", "pz", None), P("py", "px", "pz", None))
    return jax.shard_map(
        local,
        mesh=mesh,
        in_specs=placed,
        out_specs=(P("py", "px", "pz", None), P("py", "px", "pz", None)),
        check_vma=False,
    )
```

profile of v0, /device:TPU:0, one launch (start us, length us, event | category | flops | bytes accessed | tf_op | source)
XLA Modules:
  0.0 305.5 jit_solution(18165291161526020677)
XLA Ops:
  7.2 1.3 fusion.36
  8.5 3.0 collective-permute-start
  11.6 12.7 %collective-permute-done = f32[1,16,64,128]{3,2,1,0:T(8,128)S(1)} collective-permute-done((f32[1,16,64,128]{3,2,1,0:T(8,128)S(1)}, f32[1,16,64,128]{3,2,1,0:T(8,128)S(1)}, u32[]{:S(2)}, u32[]{:S(2)}) %collective-permute-start) | collective-permute-done | bytes 524320 | tf_op jit(solution)/shard_map/ppermute | solution.py:16
  24.3 2.5 constant_dynamic-update-slice_fusion.1
  26.8 7.8 %collective-permute-done.1 = f32[1,16,64,128]{3,2,1,0:T(8,128)S(1)} collective-permute-done((f32[1,16,64,128]{3,2,1,0:T(8,128)S(1)}, f32[1,16,64,128]{3,2,1,0:T(8,128)S(1)}, u32[]{:S(2)}, u32[]{:S(2)}) %collective-permute-start.1) | collective-permute-done | bytes 524320 | tf_op jit(solution)/shard_map/ppermute | solution.py:17
  34.8 1.9 collective-permute-start.2
  36.7 2.1 collective-permute-start.3
  38.8 8.5 %collective-permute-done.2 = f32[10,1,64,128]{3,2,1,0:T(8,128)S(1)} collective-permute-done((f32[10,1,64,128]{3,2,1,0:T(8,128)S(1)}, f32[10,1,64,128]{3,2,1,0:T(8,128)S(1)}, u32[]{:S(2)}, u32[]{:S(2)}) %collective-permute-start.2) | collective-permute-done | bytes 327712 | tf_op jit(solution)/shard_map/ppermute | solution.py:16
  47.3 4.7 %collective-permute-done.3 = f32[10,1,64,128]{3,2,1,0:T(8,128)S(1)} collective-permute-done((f32[10,1,64,128]{3,2,1,0:T(8,128)S(1)}, f32[10,1,64,128]{3,2,1,0:T(8,128)S(1)}, u32[]{:S(2)}, u32[]{:S(2)}) %collective-permute-start.3) | collective-permute-done | bytes 327712 | tf_op jit(solution)/shard_map/ppermute | solution.py:17
  52.0 0.1 pad_maximum_fusion.90
  52.3 1.8 collective-permute-start.5
  54.0 2.5 collective-permute-done.4
  56.6 0.3 collective-permute-done.5
  57.0 15.7 %fusion.27 = f32[8,16,64,128]{3,2,1,0:T(8,128)S(1)} fusion(f32[8,16,64,128]{3,2,1,0:T(8,128)} %param.7, f32[10,18,1,128]{3,2,1,0:T(1,128)S(1)} %copy.27, f32[10,1,64,128]{3,2,1,0:T(8,128)S(1)} %collective-permute-done.3, f32[10,16,64,128]{3,2,1,0:T(8,128)} %copy-done.3, f32[10,1,64,128]{3,2,1,0:T(8,128)S(1)} %collective-permute-done.2, ...), kind=kLoop, calls=%fused_computation.83 | loop fusion | flops 22020096 | bytes 23908352 | tf_op jit(solution)/shard_map/add | solution.py:52
  72.8 1.6 collective-permute-start.6
  74.3 0.5 collective-permute-start.7
  74.8 12.4 %collective-permute-done.6 = f32[1,16,64,128]{3,2,1,0:T(8,128)S(1)} collective-permute-done((f32[1,16,64,128]{3,2,1,0:T(8,128)S(1)}, f32[1,16,64,128]{3,2,1,0:T(8,128)S(1)}, u32[]{:S(2)}, u32[]{:S(2)}) %collective-permute-start.6) | collective-permute-done | bytes 524320 | tf_op jit(solution)/shard_map/ppermute | solution.py:16
  87.2 11.2 %collective-permute-done.7 = f32[1,16,64,128]{3,2,1,0:T(8,128)S(1)} collective-permute-done((f32[1,16,64,128]{3,2,1,0:T(8,128)S(1)}, f32[1,16,64,128]{3,2,1,0:T(8,128)S(1)}, u32[]{:S(2)}, u32[]{:S(2)}) %collective-permute-start.7) | collective-permute-done | bytes 524320 | tf_op jit(solution)/shard_map/ppermute | solution.py:17
  98.5 1.2 collective-permute-start.8
  99.7 2.7 collective-permute-start.9
  102.4 8.6 %collective-permute-done.8 = f32[10,1,64,128]{3,2,1,0:T(8,128)S(1)} collective-permute-done((f32[10,1,64,128]{3,2,1,0:T(8,128)S(1)}, f32[10,1,64,128]{3,2,1,0:T(8,128)S(1)}, u32[]{:S(2)}, u32[]{:S(2)}) %collective-permute-start.8) | collective-permute-done | bytes 327712 | tf_op jit(solution)/shard_map/ppermute | solution.py:16
  111.0 5.3 %collective-permute-done.9 = f32[10,1,64,128]{3,2,1,0:T(8,128)S(1)} collective-permute-done((f32[10,1,64,128]{3,2,1,0:T(8,128)S(1)}, f32[10,1,64,128]{3,2,1,0:T(8,128)S(1)}, u32[]{:S(2)}, u32[]{:S(2)}) %collective-permute-start.9) | collective-permute-done | bytes 327712 | tf_op jit(solution)/shard_map/ppermute | solution.py:17
  116.3 0.1 pad_maximum_fusion.87
  116.5 1.8 collective-permute-start.11
  118.3 2.5 collective-permute-done.10
  120.9 0.1 copy.31
  121.0 10.3 %fusion.19 = f32[8,16,64,128]{3,2,1,0:T(8,128)} fusion(f32[8,16,64,128]{3,2,1,0:T(8,128)} %param.7, f32[10,18,1,128]{3,2,1,0:T(1,128)S(1)} %copy.31, f32[10,1,64,128]{3,2,1,0:T(8,128)S(1)} %collective-permute-done.9, f32[10,1,64,128]{3,2,1,0:T(8,128)S(1)} %collective-permute-done.8, f32[1,16,64,128]{3,2,1,0:T(8,128)S(1)} %collective-permute-done.7, ...), kind=kLoop, calls=%fused_computation.57 | loop fusion | flops 30408704 | bytes 18665472 | tf_op jit(solution)/shard_map/add | solution.py:52
  131.3 1.4 fusion.34
  132.7 1.6 collective-permute-start.12
  134.3 0.5 collective-permute-start.13
  134.8 12.5 %collective-permute-done.12 = f32[1,16,64,128]{3,2,1,0:T(8,128)S(1)} collective-permute-done((f32[1,16,64,128]{3,2,1,0:T(8,128)S(1)}, f32[1,16,64,128]{3,2,1,0:T(8,128)S(1)}, u32[]{:S(2)}, u32[]{:S(2)}) %collective-permute-start.12) | collective-permute-done | bytes 524320 | tf_op jit(solution)/shard_map/ppermute | solution.py:16
  147.3 11.2 %collective-permute-done.13 = f32[1,16,64,128]{3,2,1,0:T(8,128)S(1)} collective-permute-done((f32[1,16,64,128]{3,2,1,0:T(8,128)S(1)}, f32[1,16,64,128]{3,2,1,0:T(8,128)S(1)}, u32[]{:S(2)}, u32[]{:S(2)}) %collective-permute-start.13) | collective-permute-done | bytes 524320 | tf_op jit(solution)/shard_map/ppermute | solution.py:17
  158.5 1.1 pad_maximum_fusion.69
  159.6 0.8 collective-permute-start.14
  160.4 3.1 %collective-permute-start.15 = (f32[10,1,64,128]{3,2,1,0:T(8,128)S(1)}, f32[10,1,64,128]{3,2,1,0:T(8,128)S(1)}, u32[]{:S(2)}, u32[]{:S(2)}) collective-permute-start(f32[10,1,64,128]{3,2,1,0:T(8,128)S(1)} %get-tuple-element.130), channel_id=1, source_target_pairs={{4,0},{8,4},{12,8},{0,12},{5,1},{9,5},{13,9},{1,13},{6,2},{10,6},{... | collective-permute-start | bytes 983048 | tf_op jit(solution)/shard_map/ppermute | solution.py:17
  163.5 8.6 %collective-permute-done.14 = f32[10,1,64,128]{3,2,1,0:T(8,128)S(1)} collective-permute-done((f32[10,1,64,128]{3,2,1,0:T(8,128)S(1)}, f32[10,1,64,128]{3,2,1,0:T(8,128)S(1)}, u32[]{:S(2)}, u32[]{:S(2)}) %collective-permute-start.14) | collective-permute-done | bytes 327712 | tf_op jit(solution)/shard_map/ppermute | solution.py:16
  172.1 4.8 %collective-permute-done.15 = f32[10,1,64,128]{3,2,1,0:T(8,128)S(1)} collective-permute-done((f32[10,1,64,128]{3,2,1,0:T(8,128)S(1)}, f32[10,1,64,128]{3,2,1,0:T(8,128)S(1)}, u32[]{:S(2)}, u32[]{:S(2)}) %collective-permute-start.15) | collective-permute-done | bytes 327712 | tf_op jit(solution)/shard_map/ppermute | solution.py:17
  176.9 0.1 pad_maximum_fusion.82
  177.1 1.8 collective-permute-start.17
  178.9 2.5 collective-permute-done.16
  181.5 0.2 collective-permute-done.17
  181.8 15.8 %fusion.11 = f32[8,16,64,128]{3,2,1,0:T(8,128)} fusion(f32[8,16,64,128]{3,2,1,0:T(8,128)} %param.7, f32[10,18,1,128]{3,2,1,0:T(1,128)S(1)} %copy.35, f32[10,1,64,128]{3,2,1,0:T(8,128)S(1)} %collective-permute-done.15, f32[10,1,64,128]{3,2,1,0:T(8,128)S(1)} %collective-permute-done.14, f32[1,16,64,128]{3,2,1,0:T(8,128)S(1)} %collective-permute-done.13, ...), kind=kLoop, calls=%fused_computation.31 | loop fusion | flops 30408704 | bytes 18665472 | tf_op jit(solution)/shard_map/add | solution.py:52
  197.6 1.4 fusion.33
  199.1 1.6 collective-permute-start.18
  200.6 0.5 collective-permute-start.19
  201.2 12.4 %collective-permute-done.18 = f32[1,16,64,128]{3,2,1,0:T(8,128)S(1)} collective-permute-done((f32[1,16,64,128]{3,2,1,0:T(8,128)S(1)}, f32[1,16,64,128]{3,2,1,0:T(8,128)S(1)}, u32[]{:S(2)}, u32[]{:S(2)}) %collective-permute-start.18) | collective-permute-done | bytes 524320 | tf_op jit(solution)/shard_map/ppermute | solution.py:16
  213.6 11.2 %collective-permute-done.19 = f32[1,16,64,128]{3,2,1,0:T(8,128)S(1)} collective-permute-done((f32[1,16,64,128]{3,2,1,0:T(8,128)S(1)}, f32[1,16,64,128]{3,2,1,0:T(8,128)S(1)}, u32[]{:S(2)}, u32[]{:S(2)}) %collective-permute-start.19) | collective-permute-done | bytes 524320 | tf_op jit(solution)/shard_map/ppermute | solution.py:17
  224.8 1.1 pad_maximum_fusion.66
  225.9 1.4 collective-permute-start.20
  227.3 2.4 collective-permute-start.21
  229.8 8.6 %collective-permute-done.20 = f32[10,1,64,128]{3,2,1,0:T(8,128)S(1)} collective-permute-done((f32[10,1,64,128]{3,2,1,0:T(8,128)S(1)}, f32[10,1,64,128]{3,2,1,0:T(8,128)S(1)}, u32[]{:S(2)}, u32[]{:S(2)}) %collective-permute-start.20) | collective-permute-done | bytes 327712 | tf_op jit(solution)/shard_map/ppermute | solution.py:16
  238.4 5.5 %collective-permute-done.21 = f32[10,1,64,128]{3,2,1,0:T(8,128)S(1)} collective-permute-done((f32[10,1,64,128]{3,2,1,0:T(8,128)S(1)}, f32[10,1,64,128]{3,2,1,0:T(8,128)S(1)}, u32[]{:S(2)}, u32[]{:S(2)}) %collective-permute-start.21) | collective-permute-done | bytes 327712 | tf_op jit(solution)/shard_map/ppermute | solution.py:17
  243.9 0.1 pad_maximum_fusion.77
  244.1 2.0 collective-permute-start.23
  246.1 2.3 collective-permute-done.22
  248.6 15.3 %fusion.3 = f32[8,16,64,128]{3,2,1,0:T(8,128)} fusion(f32[8,16,64,128]{3,2,1,0:T(8,128)} %param.7, f32[10,18,1,128]{3,2,1,0:T(1,128)S(1)} %copy.39, f32[10,1,64,128]{3,2,1,0:T(8,128)S(1)} %collective-permute-done.21, f32[10,1,64,128]{3,2,1,0:T(8,128)S(1)} %collective-permute-done.20, f32[1,16,64,128]{3,2,1,0:T(8,128)S(1)} %collective-permute-done.19, ...), kind=kLoop, calls=%fused_computation.5 | loop fusion | flops 30408704 | bytes 18665472 | tf_op jit(solution)/shard_map/add | solution.py:52
  263.9 2.6 fusion.37
  266.6 2.0 copy-done.4
  268.6 0.8 slice.360
  269.5 21.6 %all-gather.3.cloned.1.call-done = f32[2,16,64,128]{3,2,1,0:T(8,128)} async-done(((f32[1,16,64,128]{3,2,1,0:T(8,128)}), f32[2,16,64,128]{3,2,1,0:T(8,128)}) %all-gather.3.cloned.1.call-update) | async-done | bytes 1048592 | tf_op jit(solution)/shard_map/all_gather | solution.py:24
  291.0 2.5 while.14
  291.0 1.2 add_select_fusion.2
  292.3 1.2 add_select_fusion.2
  293.5 5.1 %add_multiply_fusion = f32[8,16,64,128]{3,2,1,0:T(8,128)} fusion(f32[8,16,64,128]{3,2,1,0:T(8,128)} %copy-done.4, f32[16,64,128]{2,1,0:T(8,128)S(1)} %bitcast.9), kind=kLoop, calls=%fused_computation.97 | loop fusion | flops 2097152 | bytes 8912896 | tf_op jit(solution)/shard_map/div | solution.py:67
  (39 shorter events, 1.4 us)
Async XLA Ops:
  7.2 283.9 %all-gather.3.cloned.1.call-start = ((), (), s32[]{:S(2)}) async-start(), calls=%async_computation | async-start | bytes 1572864 | tf_op jit(solution)/shard_map/all_gather | solution.py:24
  8.5 15.8 %collective-permute-start = (f32[1,16,64,128]{3,2,1,0:T(8,128)S(1)}, f32[1,16,64,128]{3,2,1,0:T(8,128)S(1)}, u32[]{:S(2)}, u32[]{:S(2)}) collective-permute-start(f32[1,16,64,128]{3,2,1,0:T(8,128)S(1)} %get-tuple-element.142), channel_id=1, source_target_pairs={{0,16},{16,0},{1,17},{17,1},{2,18},{18,2},{3,19},{19,3},{4,20},{20... | collective-permute-start | bytes 1572872 | tf_op jit(solution)/shard_map/ppermute | solution.py:16
  11.5 23.2 %collective-permute-start.1 = (f32[1,16,64,128]{3,2,1,0:T(8,128)S(1)}, f32[1,16,64,128]{3,2,1,0:T(8,128)S(1)}, u32[]{:S(2)}, u32[]{:S(2)}) collective-permute-start(f32[1,16,64,128]{3,2,1,0:T(8,128)S(1)} %get-tuple-element.141), channel_id=1, source_target_pairs={{16,0},{0,16},{17,1},{1,17},{18,2},{2,18},{19,3},{3,19},{20,4},{4,... | collective-permute-start | bytes 1572872 | tf_op jit(solution)/shard_map/ppermute | solution.py:17
  34.7 22.2 %copy-start.3 = (f32[10,16,64,128]{3,2,1,0:T(8,128)}, f32[10,16,64,128]{3,2,1,0:T(8,128)S(1)}, u32[]{:S(2)}) copy-start(f32[10,16,64,128]{3,2,1,0:T(8,128)S(1)} %constant_dynamic-update-slice_fusion) | copy-start | bytes 15728644
  34.8 12.5 %collective-permute-start.2 = (f32[10,1,64,128]{3,2,1,0:T(8,128)S(1)}, f32[10,1,64,128]{3,2,1,0:T(8,128)S(1)}, u32[]{:S(2)}, u32[]{:S(2)}) collective-permute-start(f32[10,1,64,128]{3,2,1,0:T(8,128)S(1)} %get-tuple-element.133), channel_id=1, source_target_pairs={{0,4},{4,8},{8,12},{12,0},{1,5},{5,9},{9,13},{13,1},{2,6},{6,10},{... | collective-permute-start | bytes 983048 | tf_op jit(solution)/shard_map/ppermute | solution.py:16
  36.7 15.3 %collective-permute-start.3 = (f32[10,1,64,128]{3,2,1,0:T(8,128)S(1)}, f32[10,1,64,128]{3,2,1,0:T(8,128)S(1)}, u32[]{:S(2)}, u32[]{:S(2)}) collective-permute-start(f32[10,1,64,128]{3,2,1,0:T(8,128)S(1)} %get-tuple-element.134), channel_id=1, source_target_pairs={{4,0},{8,4},{12,8},{0,12},{5,1},{9,5},{13,9},{1,13},{6,2},{10,6},{... | collective-permute-start | bytes 983048 | tf_op jit(solution)/shard_map/ppermute | solution.py:17
  52.2 4.4 %collective-permute-start.4 = (f32[10,18,1,128]{3,1,2,0:T(8,128)S(1)}, f32[10,18,1,128]{3,1,2,0:T(8,128)S(1)}, u32[]{:S(2)}, u32[]{:S(2)}) collective-permute-start(f32[10,18,1,128]{3,1,2,0:T(8,128)S(1)} %copy.24), channel_id=1, source_target_pairs={{0,1},{1,2},{2,3},{3,0},{4,5},{5,6},{6,7},{7,4},{8,9},{9,10},{10,1... | collective-permute-start | bytes 276488 | tf_op jit(solution)/shard_map/ppermute | solution.py:16
  52.3 4.6 %collective-permute-start.5 = (f32[10,18,1,128]{3,1,2,0:T(8,128)S(1)}, f32[10,18,1,128]{3,1,2,0:T(8,128)S(1)}, u32[]{:S(2)}, u32[]{:S(2)}) collective-permute-start(f32[10,18,1,128]{3,1,2,0:T(8,128)S(1)} %copy.26), channel_id=1, source_target_pairs={{1,0},{2,1},{3,2},{0,3},{5,4},{6,5},{7,6},{4,7},{9,8},{10,9},{11,1... | collective-permute-start | bytes 276488 | tf_op jit(solution)/shard_map/ppermute | solution.py:17
  72.8 14.5 %collective-permute-start.6 = (f32[1,16,64,128]{3,2,1,0:T(8,128)S(1)}, f32[1,16,64,128]{3,2,1,0:T(8,128)S(1)}, u32[]{:S(2)}, u32[]{:S(2)}) collective-permute-start(f32[1,16,64,128]{3,2,1,0:T(8,128)S(1)} %get-tuple-element.139), channel_id=1, source_target_pairs={{0,16},{16,0},{1,17},{17,1},{2,18},{18,2},{3,19},{19,3},{4,20},{20... | collective-permute-start | bytes 1572872 | tf_op jit(solution)/shard_map/ppermute | solution.py:16
  74.3 24.2 %collective-permute-start.7 = (f32[1,16,64,128]{3,2,1,0:T(8,128)S(1)}, f32[1,16,64,128]{3,2,1,0:T(8,128)S(1)}, u32[]{:S(2)}, u32[]{:S(2)}) collective-permute-start(f32[1,16,64,128]{3,2,1,0:T(8,128)S(1)} %get-tuple-element.140), channel_id=1, source_target_pairs={{16,0},{0,16},{17,1},{1,17},{18,2},{2,18},{19,3},{3,19},{20,4},{4,... | collective-permute-start | bytes 1572872 | tf_op jit(solution)/shard_map/ppermute | solution.py:17
  98.5 12.5 %collective-permute-start.8 = (f32[10,1,64,128]{3,2,1,0:T(8,128)S(1)}, f32[10,1,64,128]{3,2,1,0:T(8,128)S(1)}, u32[]{:S(2)}, u32[]{:S(2)}) collective-permute-start(f32[10,1,64,128]{3,2,1,0:T(8,128)S(1)} %get-tuple-element.131), channel_id=1, source_target_pairs={{0,4},{4,8},{8,12},{12,0},{1,5},{5,9},{9,13},{13,1},{2,6},{6,10},{... | collective-permute-start | bytes 983048 | tf_op jit(solution)/shard_map/ppermute | solution.py:16
  99.7 16.6 %collective-permute-start.9 = (f32[10,1,64,128]{3,2,1,0:T(8,128)S(1)}, f32[10,1,64,128]{3,2,1,0:T(8,128)S(1)}, u32[]{:S(2)}, u32[]{:S(2)}) collective-permute-start(f32[10,1,64,128]{3,2,1,0:T(8,128)S(1)} %get-tuple-element.132), channel_id=1, source_target_pairs={{4,0},{8,4},{12,8},{0,12},{5,1},{9,5},{13,9},{1,13},{6,2},{10,6},{... | collective-permute-start | bytes 983048 | tf_op jit(solution)/shard_map/ppermute | solution.py:17
  116.4 4.4 %collective-permute-start.10 = (f32[10,18,1,128]{3,1,2,0:T(8,128)S(1)}, f32[10,18,1,128]{3,1,2,0:T(8,128)S(1)}, u32[]{:S(2)}, u32[]{:S(2)}) collective-permute-start(f32[10,18,1,128]{3,1,2,0:T(8,128)S(1)} %copy.28), channel_id=1, source_target_pairs={{0,1},{1,2},{2,3},{3,0},{4,5},{5,6},{6,7},{7,4},{8,9},{9,10},{10,1... | collective-permute-start | bytes 276488 | tf_op jit(solution)/shard_map/ppermute | solution.py:16
  116.5 4.4 %collective-permute-start.11 = (f32[10,18,1,128]{3,1,2,0:T(8,128)S(1)}, f32[10,18,1,128]{3,1,2,0:T(8,128)S(1)}, u32[]{:S(2)}, u32[]{:S(2)}) collective-permute-start(f32[10,18,1,128]{3,1,2,0:T(8,128)S(1)} %copy.30), channel_id=1, source_target_pairs={{1,0},{2,1},{3,2},{0,3},{5,4},{6,5},{7,6},{4,7},{9,8},{10,9},{11,1... | collective-permute-start | bytes 276488 | tf_op jit(solution)/shard_map/ppermute | solution.py:17
  131.3 45.6 %copy-start = (f32[8,16,64,128]{3,2,1,0:T(8,128)S(1)}, f32[8,16,64,128]{3,2,1,0:T(8,128)}, u32[]{:S(2)}) copy-start(f32[8,16,64,128]{3,2,1,0:T(8,128)} %fusion.19) | copy-start | bytes 12582916
  132.7 14.5 %collective-permute-start.12 = (f32[1,16,64,128]{3,2,1,0:T(8,128)S(1)}, f32[1,16,64,128]{3,2,1,0:T(8,128)S(1)}, u32[]{:S(2)}, u32[]{:S(2)}) collective-permute-start(f32[1,16,64,128]{3,2,1,0:T(8,128)S(1)} %get-tuple-element.137), channel_id=1, source_target_pairs={{0,16},{16,0},{1,17},{17,1},{2,18},{18,2},{3,19},{19,3},{4,20},{20... | collective-permute-start | bytes 1572872 | tf_op jit(solution)/shard_map/ppermute | solution.py:16
  134.3 24.2 %collective-permute-start.13 = (f32[1,16,64,128]{3,2,1,0:T(8,128)S(1)}, f32[1,16,64,128]{3,2,1,0:T(8,128)S(1)}, u32[]{:S(2)}, u32[]{:S(2)}) collective-permute-start(f32[1,16,64,128]{3,2,1,0:T(8,128)S(1)} %get-tuple-element.138), channel_id=1, source_target_pairs={{16,0},{0,16},{17,1},{1,17},{18,2},{2,18},{19,3},{3,19},{20,4},{4,... | collective-permute-start | bytes 1572872 | tf_op jit(solution)/shard_map/ppermute | solution.py:17
  159.6 12.5 %collective-permute-start.14 = (f32[10,1,64,128]{3,2,1,0:T(8,128)S(1)}, f32[10,1,64,128]{3,2,1,0:T(8,128)S(1)}, u32[]{:S(2)}, u32[]{:S(2)}) collective-permute-start(f32[10,1,64,128]{3,2,1,0:T(8,128)S(1)} %get-tuple-element.129), channel_id=1, source_target_pairs={{0,4},{4,8},{8,12},{12,0},{1,5},{5,9},{9,13},{13,1},{2,6},{6,10},{... | collective-permute-start | bytes 983048 | tf_op jit(solution)/shard_map/ppermute | solution.py:16
  160.4 16.5 %collective-permute-start.15 = (f32[10,1,64,128]{3,2,1,0:T(8,128)S(1)}, f32[10,1,64,128]{3,2,1,0:T(8,128)S(1)}, u32[]{:S(2)}, u32[]{:S(2)}) collective-permute-start(f32[10,1,64,128]{3,2,1,0:T(8,128)S(1)} %get-tuple-element.130), channel_id=1, source_target_pairs={{4,0},{8,4},{12,8},{0,12},{5,1},{9,5},{13,9},{1,13},{6,2},{10,6},{... | collective-permute-start | bytes 983048 | tf_op jit(solution)/shard_map/ppermute | solution.py:17
  177.0 4.4 %collective-permute-start.16 = (f32[10,18,1,128]{3,1,2,0:T(8,128)S(1)}, f32[10,18,1,128]{3,1,2,0:T(8,128)S(1)}, u32[]{:S(2)}, u32[]{:S(2)}) collective-permute-start(f32[10,18,1,128]{3,1,2,0:T(8,128)S(1)} %copy.32), channel_id=1, source_target_pairs={{0,1},{1,2},{2,3},{3,0},{4,5},{5,6},{6,7},{7,4},{8,9},{9,10},{10,1... | collective-permute-start | bytes 276488 | tf_op jit(solution)/shard_map/ppermute | solution.py:16
  177.1 4.6 %collective-permute-start.17 = (f32[10,18,1,128]{3,1,2,0:T(8,128)S(1)}, f32[10,18,1,128]{3,1,2,0:T(8,128)S(1)}, u32[]{:S(2)}, u32[]{:S(2)}) collective-permute-start(f32[10,18,1,128]{3,1,2,0:T(8,128)S(1)} %copy.34), channel_id=1, source_target_pairs={{1,0},{2,1},{3,2},{0,3},{5,4},{6,5},{7,6},{4,7},{9,8},{10,9},{11,1... | collective-permute-start | bytes 276488 | tf_op jit(solution)/shard_map/ppermute | solution.py:17
  197.6 46.3 %copy-start.2 = (f32[8,16,64,128]{3,2,1,0:T(8,128)S(1)}, f32[8,16,64,128]{3,2,1,0:T(8,128)}, u32[]{:S(2)}) copy-start(f32[8,16,64,128]{3,2,1,0:T(8,128)} %fusion.11) | copy-start | bytes 12582916
  199.1 14.5 %collective-permute-start.18 = (f32[1,16,64,128]{3,2,1,0:T(8,128)S(1)}, f32[1,16,64,128]{3,2,1,0:T(8,128)S(1)}, u32[]{:S(2)}, u32[]{:S(2)}) collective-permute-start(f32[1,16,64,128]{3,2,1,0:T(8,128)S(1)} %get-tuple-element.135), channel_id=1, source_target_pairs={{0,16},{16,0},{1,17},{17,1},{2,18},{18,2},{3,19},{19,3},{4,20},{20... | collective-permute-start | bytes 1572872 | tf_op jit(solution)/shard_map/ppermute | solution.py:16
  200.6 24.2 %collective-permute-start.19 = (f32[1,16,64,128]{3,2,1,0:T(8,128)S(1)}, f32[1,16,64,128]{3,2,1,0:T(8,128)S(1)}, u32[]{:S(2)}, u32[]{:S(2)}) collective-permute-start(f32[1,16,64,128]{3,2,1,0:T(8,128)S(1)} %get-tuple-element.136), channel_id=1, source_target_pairs={{16,0},{0,16},{17,1},{1,17},{18,2},{2,18},{19,3},{3,19},{20,4},{4,... | collective-permute-start | bytes 1572872 | tf_op jit(solution)/shard_map/ppermute | solution.py:17
  225.9 22.8 %copy-start.1 = (f32[8,16,64,128]{3,2,1,0:T(8,128)S(1)}, f32[8,16,64,128]{3,2,1,0:T(8,128)}, u32[]{:S(2)}) copy-start(f32[8,16,64,128]{3,2,1,0:T(8,128)} %fusion.19) | copy-start | bytes 12582916
  225.9 12.5 %collective-permute-start.20 = (f32[10,1,64,128]{3,2,1,0:T(8,128)S(1)}, f32[10,1,64,128]{3,2,1,0:T(8,128)S(1)}, u32[]{:S(2)}, u32[]{:S(2)}) collective-permute-start(f32[10,1,64,128]{3,2,1,0:T(8,128)S(1)} %get-tuple-element.127), channel_id=1, source_target_pairs={{0,4},{4,8},{8,12},{12,0},{1,5},{5,9},{9,13},{13,1},{2,6},{6,10},{... | collective-permute-start | bytes 983048 | tf_op jit(solution)/shard_map/ppermute | solution.py:16
  227.3 16.6 %collective-permute-start.21 = (f32[10,1,64,128]{3,2,1,0:T(8,128)S(1)}, f32[10,1,64,128]{3,2,1,0:T(8,128)S(1)}, u32[]{:S(2)}, u32[]{:S(2)}) collective-permute-start(f32[10,1,64,128]{3,2,1,0:T(8,128)S(1)} %get-tuple-element.128), channel_id=1, source_target_pairs={{4,0},{8,4},{12,8},{0,12},{5,1},{9,5},{13,9},{1,13},{6,2},{10,6},{... | collective-permute-start | bytes 983048 | tf_op jit(solution)/shard_map/ppermute | solution.py:17
  244.0 4.4 %collective-permute-start.22 = (f32[10,18,1,128]{3,1,2,0:T(8,128)S(1)}, f32[10,18,1,128]{3,1,2,0:T(8,128)S(1)}, u32[]{:S(2)}, u32[]{:S(2)}) collective-permute-start(f32[10,18,1,128]{3,1,2,0:T(8,128)S(1)} %copy.36), channel_id=1, source_target_pairs={{0,1},{1,2},{2,3},{3,0},{4,5},{5,6},{6,7},{7,4},{8,9},{9,10},{10,1... | collective-permute-start | bytes 276488 | tf_op jit(solution)/shard_map/ppermute | solution.py:16
  244.1 4.4 %collective-permute-start.23 = (f32[10,18,1,128]{3,1,2,0:T(8,128)S(1)}, f32[10,18,1,128]{3,1,2,0:T(8,128)S(1)}, u32[]{:S(2)}, u32[]{:S(2)}) collective-permute-start(f32[10,18,1,128]{3,1,2,0:T(8,128)S(1)} %copy.38), channel_id=1, source_target_pairs={{1,0},{2,1},{3,2},{0,3},{5,4},{6,5},{7,6},{4,7},{9,8},{10,9},{11,1... | collective-permute-start | bytes 276488 | tf_op jit(solution)/shard_map/ppermute | solution.py:17
  266.6 2.0 copy-start.4
Sparse Core Ops, SparseCore 0:
  269.6 21.4 all-gather.2
where the time goes:
time: 306 us
  waiting for transfers between devices  178 us (58%)
  other arithmetic  70 us (23%)
  starting transfers between devices  32.5 us (11%)
  between operations  14.3 us (5%)
  local copies, waits for them, and re-layouts  10.6 us (3%)
    ppermute x12, waiting for transfers between devices, with_halo(): before = lax.ppermute(last, axis, up)  94.1 us
    ppermute x12, waiting for transfers between devices, with_halo(): after = lax.ppermute(initial, axis, down)  62.3 us
    add x4, other arithmetic, march_step(): return 2.0 * middle - before + speed_square * spread  57.1 us
    all_gather x1, waiting for transfers between devices, prefix(): everything = lax.all_gather(value, axis)  21.6 us
    ppermute x12, starting transfers between devices, with_halo(): after = lax.ppermute(initial, axis, down)  19.3 us
    ppermute x12, starting transfers between devices, with_halo(): before = lax.ppermute(last, axis, up)  13.2 us
  transfers between devices with their start and end apart: 25, of which 23 were waited for; matrix products, arithmetic and copies ran while one was open for 1% of the time, Pallas kernels for 0%

commit v1 on v0

v1 whole, which is shorter than its diff:
```python
import functools

import jax
import jax.numpy as jnp
from jax import lax
from jax.experimental import pallas as pl
from jax.experimental.pallas import tpu as pltpu
from jax.sharding import PartitionSpec as P

STEPS = 4
CHUNKS = 4
MESH = pl.DeviceIdType.MESH


def march_kernel(
    peers, chunks, field, before, speed, sums_out, field_out,
    u, cs, csum, total, acc, below, ysend, yrecv,
    load_sem, x_send, x_recv, z_send, z_recv, y_send, y_recv, t_send, t_recv, out_sem, sum_sem,
):
    J, I, K, L = field.shape
    ny, nx, nz = peers
    width = I // chunks
    my, mx, mz = (lax.axis_index(a) for a in ("py", "px", "pz"))
    y_side = ({"py": lax.rem(my + 1, ny)}, {"py": lax.rem(my + ny - 1, ny)})
    x_side = ({"px": lax.rem(mx + 1, nx)}, {"px": lax.rem(mx + nx - 1, nx)})
    z_side = ({"pz": lax.rem(mz + 1, nz)}, {"pz": lax.rem(mz + nz - 1, nz)})
    parts = ((1, J - 2), (0, 1), (J - 1, 1))

    loads = [
        pltpu.make_async_copy(field, u.at[0, pl.ds(1, J), pl.ds(1, I)], load_sem.at[0]),
        pltpu.make_async_copy(before, u.at[1, pl.ds(1, J), pl.ds(1, I)], load_sem.at[1]),
        pltpu.make_async_copy(speed, cs, load_sem.at[2]),
    ]
    for load in loads:
        load.start()

    barrier = pltpu.get_barrier_semaphore()
    for d in range(1, ny):
        pl.semaphore_signal(barrier, inc=1, device_id={"py": lax.rem(my + d, ny)}, device_id_type=MESH)
    for side in x_side + z_side:
        pl.semaphore_signal(barrier, inc=1, device_id=side, device_id_type=MESH)
    pl.semaphore_wait(barrier, ny - 1 + 4)

    def remote(src, dst, send, recv, to):
        return pltpu.make_async_remote_copy(
            src_ref=src, dst_ref=dst, send_sem=send, recv_sem=recv, device_id=to, device_id_type=MESH
        )

    def j_copy(t, side, c):
        row, rim = ((J - 1, 0), (0, J + 1))[side]
        here = pl.ds(c * width, width)
        there = pl.ds(1 + c * width, width)
        src = field.at[row, here] if t == 0 else u.at[t % 2, row + 1, there]
        return remote(src, u.at[t % 2, rim, there], x_send.at[t, side, c], x_recv.at[t, side, c], y_side[side])

    def i_copy(t, side, part):
        plane, rim = ((I - 1, 0), (0, I + 1))[side]
        start, size = parts[part]
        rows = pl.ds(start + 1, size)
        src = field.at[pl.ds(start, size), plane] if t == 0 else u.at[t % 2, rows, plane + 1]
        return remote(src, u.at[t % 2, rows, rim], z_send.at[t, side, part], z_recv.at[t, side, part], x_side[side])

    def k_copy(t, side, part):
        start, size = parts[part]
        rows = pl.ds(start, size)
        return remote(
            ysend.at[t, side, rows], yrecv.at[t, side, rows],
            y_send.at[t, side, part], y_recv.at[t, side, part], z_side[side],
        )

    def pack(t, j, i, value):
        ysend[t, 0, j, pl.ds(i, 1), :] = value[K - 1:K]
        ysend[t, 1, j, pl.ds(i, 1), :] = value[0:1]

    for c in range(chunks):
        for side in (0, 1):
            j_copy(0, side, c).start()
    for part in range(3):
        for side in (0, 1):
            i_copy(0, side, part).start()

    loads[0].wait()

    def pack_row(j, carry):
        for i in range(I):
            ysend[0, 0, j, i:i + 1, :] = u[0, j + 1, i + 1, K - 1:K, :]
            ysend[0, 1, j, i:i + 1, :] = u[0, j + 1, i + 1, 0:1, :]
        return carry

    lax.fori_loop(0, J, pack_row, 0)
    for part in range(3):
        for side in (0, 1):
            k_copy(0, side, part).start()
    loads[1].wait()
    loads[2].wait()

    k_index = lax.broadcasted_iota(jnp.int32, (K, L), 0)

    def column(t, j, i):
        now, other = t % 2, (t + 1) % 2
        middle = u[now, j + 1, i + 1]
        low = jnp.where(k_index == 0, yrecv[t, 0, j, pl.ds(i, 1), :], pltpu.roll(middle, 1, 0))
        high = jnp.where(k_index == K - 1, yrecv[t, 1, j, pl.ds(i, 1), :], pltpu.roll(middle, K - 1, 0))
        spread = (
            u[now, j, i + 1] + u[now, j + 2, i + 1] + u[now, j + 1, i] + u[now, j + 1, i + 2]
            + low + high - 6.0 * middle
        )
        later = 2.0 * middle - u[other, j + 1, i + 1] + cs[j, i] * spread
        u[other, j + 1, i + 1] = later
        if t + 1 < STEPS:
            pack(t + 1, j, i, later)

    def out_copy(part, c):
        start, size = parts[part]
        here = pl.ds(0, I) if part == 0 else pl.ds(c * width, width)
        there = pl.ds(1, I) if part == 0 else pl.ds(1 + c * width, width)
        rows = pl.ds(start, size)
        return pltpu.make_async_copy(
            u.at[STEPS % 2, pl.ds(start + 1, size), there], field_out.at[rows, here], out_sem.at[part, c]
        )

    def total_copy(d, c):
        here = pl.ds(c * width, width)
        return remote(
            total.at[here], below.at[d - 1, here], t_send.at[d - 1, c], t_recv.at[d - 1, c],
            {"py": lax.rem(my + d, ny)},
        )

    for t in range(STEPS):
        last = t + 1 == STEPS
        for side in (0, 1):
            i_copy(t, side, 0).wait_recv()
            k_copy(t, side, 0).wait_recv()
            if t > 0:
                i_copy(t - 1, side, 0).wait_send()

        def inner(q, carry, t=t):
            j = 1 + q // (I // 2)
            i = lax.rem(q, I // 2) * 2
            column(t, j, i)
            column(t, j, i + 1)
            return carry

        lax.fori_loop(0, (J - 2) * (I // 2), inner, 0)
        if not last:
            for side in (0, 1):
                i_copy(t + 1, side, 0).start()
                k_copy(t + 1, side, 0).start()
        else:
            out_copy(0, 0).start()

        for side in (0, 1):
            for part in (1, 2):
                i_copy(t, side, part).wait_recv()
                k_copy(t, side, part).wait_recv()
                if t > 0:
                    i_copy(t - 1, side, part).wait_send()
        for c in range(chunks):
            for side in (0, 1):
                j_copy(t, side, c).wait_recv()
                if t > 0:
                    j_copy(t - 1, side, c).wait_send()

            def outer(q, carry, t=t, c=c):
                i = c * width + q
                column(t, 0, i)
                column(t, J - 1, i)
                return carry

            lax.fori_loop(0, width, outer, 0)
            if not last:
                for side in (0, 1):
                    j_copy(t + 1, side, c).start()
            else:
                def add_up(q, carry, c=c):
                    i = c * width + q
                    value = u[STEPS % 2, 1, i + 1]
                    for j in range(1, J):
                        value = value + u[STEPS % 2, j + 1, i + 1]
                    total[i] = value
                    return carry

                lax.fori_loop(0, width, add_up, 0)
                for d in range(1, ny):
                    @pl.when(my + d < ny)
                    def _(d=d, c=c):
                        total_copy(d, c).start()
                for part in (1, 2):
                    out_copy(part, c).start()
        if not last:
            for part in (1, 2):
                for side in (0, 1):
                    i_copy(t + 1, side, part).start()
                    k_copy(t + 1, side, part).start()

    scale = 1.0 / (J * ny)

    def sum_copy(c):
        here = pl.ds(c * width, width)
        return pltpu.make_async_copy(csum.at[:, here], sums_out.at[:, here], sum_sem.at[c])

    for c in range(chunks):
        here = pl.ds(c * width, width)
        acc[...] = jnp.zeros_like(acc)
        for d in range(1, ny):
            @pl.when(my >= d)
            def _(d=d, c=c, here=here):
                total_copy(d, c).wait_recv()
                acc[...] = acc[...] + below[d - 1, here]

        def running(q, carry, c=c):
            i = c * width + q
            value = acc[q]
            for j in range(J):
                value = value + u[STEPS % 2, j + 1, i + 1]
                csum[j, i] = value * scale
            return carry

        lax.fori_loop(0, width, running, 0)
        sum_copy(c).start()

    for side in (0, 1):
        for c in range(chunks):
            j_copy(STEPS - 1, side, c).wait_send()
        for part in range(3):
            i_copy(STEPS - 1, side, part).wait_send()
            for t in range(STEPS):
                k_copy(t, side, part).wait_send()
    for c in range(chunks):
        for d in range(1, ny):
            @pl.when(my + d < ny)
            def _(d=d, c=c):
                total_copy(d, c).wait_send()
        for part in (1, 2):
            out_copy(part, c).wait()
        sum_copy(c).wait()
    out_copy(0, 0).wait()


def local(peers, field_now, earlier, speed_square):
    J, I, K, L = field_now.shape
    chunks = CHUNKS if I % CHUNKS == 0 else 1
    ny = peers[0]
    f32 = jnp.float32
    dma = pltpu.SemaphoreType.DMA
    anywhere = pl.BlockSpec(memory_space=pltpu.MemorySpace.HBM)
    shape = jax.ShapeDtypeStruct(field_now.shape, f32)
    slots = max(ny - 1, 1)
    return pl.pallas_call(
        functools.partial(march_kernel, peers, chunks),
        out_shape=(shape, shape),
        in_specs=[anywhere] * 3,
        out_specs=(anywhere, anywhere),
        scratch_shapes=[
            pltpu.VMEM((2, J + 2, I + 2, K, L), f32),
            pltpu.VMEM((J, I, K, L), f32),
            pltpu.VMEM((J, I, K, L), f32),
            pltpu.VMEM((I, K, L), f32),
            pltpu.VMEM((I // chunks, K, L), f32),
            pltpu.VMEM((slots, I, K, L), f32),
            pltpu.VMEM((STEPS, 2, J, I, L), f32),
            pltpu.VMEM((STEPS, 2, J, I, L), f32),
            dma((3,)),
            dma((STEPS, 2, chunks)),
            dma((STEPS, 2, chunks)),
            dma((STEPS, 2, 3)),
            dma((STEPS, 2, 3)),
            dma((STEPS, 2, 3)),
            dma((STEPS, 2, 3)),
            dma((slots, chunks)),
            dma((slots, chunks)),
            dma((3, chunks)),
            dma((chunks,)),
        ],
        compiler_params=pltpu.CompilerParams(
            collective_id=0, has_side_effects=True, vmem_limit_bytes=60 * 1024 * 1024
        ),
        name="march",
    )(field_now, earlier, speed_square)


def solution(mesh):
    placed = P("py", "px", "pz", None)
    peers = tuple(mesh.shape[a] for a in ("py", "px", "pz"))
    return jax.shard_map(
        functools.partial(local, peers),
        mesh=mesh,
        in_specs=(placed,) * 3,
        out_specs=(placed,) * 2,
        check_vma=False,
    )
```

time: 306 us -> 116 us (0.38)
  waiting for transfers between devices: 178 us -> 0 us
  Pallas kernels: 0 us -> 108 us
  other arithmetic: 70 us -> 0 us
  starting transfers between devices: 32.5 us -> 0 us
  between operations: 14.3 us -> 0.65 us
  local copies, waits for them, and re-layouts: 10.6 us -> 6.96 us
    ppermute x24 -> x0, waiting for transfers between devices: 156 us -> none  [the longest x12 94.1 us: with_halo(): before = lax.ppermute(last, axis, up)]
    pallas_call x0 -> x1, Pallas kernels: none -> 108 us  [local(): pl.pallas_call(functools.partial(march_kernel, peers, chunks), out_shape=...]
    add x4 -> x0, other arithmetic: 57.1 us -> none  [march_step(): return 2.0 * middle - before + speed_square * spread]
    ppermute x24 -> x0, starting transfers between devices: 32.5 us -> none  [the longest x12 19.3 us: with_halo(): after = lax.ppermute(initial, axis, down)]
    all_gather x1 -> x0, waiting for transfers between devices: 21.6 us -> none  [prefix(): everything = lax.all_gather(value, axis)]
    slice x14 -> x0, local copies, waits for them, and re-layouts: 5.23 us -> none  [the longest x8 3.07 us: with_halo(): last = lax.slice_in_dim(value, length - width, length, axis=dim)]
    div x1 -> x0, other arithmetic: 5.13 us -> none  [local(): column_sum = (here + below) / (field_now.shape[0] * lax.axis_size('py'))]
    unnamed x12 -> x4, local copies, waits for them, and re-layouts: 4.56 us -> 6.96 us
  transfers between devices with their start and end apart: 25 -> 0, of which waited for: 23 -> 0; matrix products, arithmetic and copies ran while one was open for 1% -> 0% of each run, Pallas kernels for 0% -> 0%
where the time goes in v1:
time: 116 us
  Pallas kernels  108 us (93%)
  local copies, waits for them, and re-layouts  6.96 us (6%)
    pallas_call x1, Pallas kernels, local(): pl.pallas_call(functools.partial(march_kernel, peers, chunks), out_shape=...  108 us
    unnamed x4, local copies, waits for them, and re-layouts  6.96 us

profile of v1, /device:TPU:0, one launch (start us, length us, event | category | flops | bytes accessed | tf_op | source)
XLA Modules:
  0.0 115.7 jit_solution(3007929626270102459)
XLA Ops:
  0.6 108.1 %march.1 = (f32[8,16,64,128]{3,2,1,0:T(8,128)}, f32[8,16,64,128]{3,2,1,0:T(8,128)}) custom-call(f32[8,16,64,128]{3,2,1,0:T(8,128)} %field.1, f32[8,16,64,128]{3,2,1,0:T(8,128)} %before.1, f32[8,16,64,128]{3,2,1,0:T(8,128)} %speed.1), custom_call_target="tpu_custom_call" | custom-call | tf_op jit(solution)/shard_map/march/pallas_call | solution.py:249
  108.7 0.0 copy-start
  108.7 4.9 %copy.7 = f32[8,16,64,128]{3,2,1,0:T(8,128)} copy(f32[8,16,64,128]{3,2,1,0:T(8,128)} %get-tuple-element.4) | data formatting | bytes 8388608
  113.7 0.0 copy-done
  113.7 2.0 %copy.8 = f32[8,16,64,128]{3,2,1,0:T(8,128)} copy(f32[8,16,64,128]{3,2,1,0:T(8,128)S(1)} %copy-done) | data formatting | bytes 8388608
Async XLA Ops:
  108.7 5.0 %copy-start = (f32[8,16,64,128]{3,2,1,0:T(8,128)S(1)}, f32[8,16,64,128]{3,2,1,0:T(8,128)}, u32[]{:S(2)}) copy-start(f32[8,16,64,128]{3,2,1,0:T(8,128)} %get-tuple-element.5) | copy-start | bytes 12582916

commit v2 on v1

--- a/solution.py
+++ b/solution.py
@@ -13,9 +13,9 @@
 
 
 def march_kernel(
-    peers, chunks, field, before, speed, sums_out, field_out,
-    u, cs, csum, total, acc, below, ysend, yrecv,
-    load_sem, x_send, x_recv, z_send, z_recv, y_send, y_recv, t_send, t_recv, out_sem, sum_sem,
+    peers, chunks, field, before, speed, end, under,
+    u, cs, total, below, ysend, yrecv,
+    load_sem, x_send, x_recv, z_send, z_recv, y_send, y_recv, t_send, t_recv,
 ):
     J, I, K, L = field.shape
     ny, nx, nz = peers
@@ -27,9 +27,13 @@
     parts = ((1, J - 2), (0, 1), (J - 1, 1))
 
     loads = [
-        pltpu.make_async_copy(field, u.at[0, pl.ds(1, J), pl.ds(1, I)], load_sem.at[0]),
-        pltpu.make_async_copy(before, u.at[1, pl.ds(1, J), pl.ds(1, I)], load_sem.at[1]),
-        pltpu.make_async_copy(speed, cs, load_sem.at[2]),
+        pltpu.make_async_copy(
+            field.at[pl.ds(start, size)], u.at[0, pl.ds(start + 1, size), pl.ds(1, I)], load_sem.at[part]
+        )
+        for part, (start, size) in reversed(tuple(enumerate(parts)))
+    ] + [
+        pltpu.make_async_copy(before, u.at[1, pl.ds(1, J), pl.ds(1, I)], load_sem.at[3]),
+        pltpu.make_async_copy(speed, cs, load_sem.at[4]),
     ]
     for load in loads:
         load.start()
@@ -48,10 +52,8 @@
 
     def j_copy(t, side, c):
         row, rim = ((J - 1, 0), (0, J + 1))[side]
-        here = pl.ds(c * width, width)
         there = pl.ds(1 + c * width, width)
-        src = field.at[row, here] if t == 0 else u.at[t % 2, row + 1, there]
-        return remote(src, u.at[t % 2, rim, there], x_send.at[t, side, c], x_recv.at[t, side, c], y_side[side])
+        return remote(u.at[t % 2, row + 1, there], u.at[t % 2, rim, there], x_send.at[t, side, c], x_recv.at[t, side, c], y_side[side])
 
     def i_copy(t, side, part):
         plane, rim = ((I - 1, 0), (0, I + 1))[side]
@@ -72,6 +74,8 @@
         ysend[t, 0, j, pl.ds(i, 1), :] = value[K - 1:K]
         ysend[t, 1, j, pl.ds(i, 1), :] = value[0:1]
 
+    for side in (0, 1):
+        loads[side].wait()
     for c in range(chunks):
         for side in (0, 1):
             j_copy(0, side, c).start()
@@ -79,7 +83,7 @@
         for side in (0, 1):
             i_copy(0, side, part).start()
 
-    loads[0].wait()
+    loads[2].wait()
 
     def pack_row(j, carry):
         for i in range(I):
@@ -91,8 +95,8 @@
     for part in range(3):
         for side in (0, 1):
             k_copy(0, side, part).start()
-    loads[1].wait()
-    loads[2].wait()
+    loads[3].wait()
+    loads[4].wait()
 
     k_index = lax.broadcasted_iota(jnp.int32, (K, L), 0)
 
@@ -106,18 +110,11 @@
             + low + high - 6.0 * middle
         )
         later = 2.0 * middle - u[other, j + 1, i + 1] + cs[j, i] * spread
-        u[other, j + 1, i + 1] = later
         if t + 1 < STEPS:
+            u[other, j + 1, i + 1] = later
             pack(t + 1, j, i, later)
-
-    def out_copy(part, c):
-        start, size = parts[part]
-        here = pl.ds(0, I) if part == 0 else pl.ds(c * width, width)
-        there = pl.ds(1, I) if part == 0 else pl.ds(1 + c * width, width)
-        rows = pl.ds(start, size)
-        return pltpu.make_async_copy(
-            u.at[STEPS % 2, pl.ds(start + 1, size), there], field_out.at[rows, here], out_sem.at[part, c]
-        )
+        else:
+            end[j, i] = later
 
     def total_copy(d, c):
         here = pl.ds(c * width, width)
@@ -146,8 +143,6 @@
             for side in (0, 1):
                 i_copy(t + 1, side, 0).start()
                 k_copy(t + 1, side, 0).start()
-        else:
-            out_copy(0, 0).start()
 
         for side in (0, 1):
             for part in (1, 2):
@@ -174,9 +169,9 @@
             else:
                 def add_up(q, carry, c=c):
                     i = c * width + q
-                    value = u[STEPS % 2, 1, i + 1]
+                    value = end[0, i]
                     for j in range(1, J):
-                        value = value + u[STEPS % 2, j + 1, i + 1]
+                        value = value + end[j, i]
                     total[i] = value
                     return carry
 
@@ -185,39 +180,20 @@
                     @pl.when(my + d < ny)
                     def _(d=d, c=c):
                         total_copy(d, c).start()
-                for part in (1, 2):
-                    out_copy(part, c).start()
         if not last:
             for part in (1, 2):
                 for side in (0, 1):
                     i_copy(t + 1, side, part).start()
                     k_copy(t + 1, side, part).start()
 
-    scale = 1.0 / (J * ny)
-
-    def sum_copy(c):
-        here = pl.ds(c * width, width)
-        return pltpu.make_async_copy(csum.at[:, here], sums_out.at[:, here], sum_sem.at[c])
-
-    for c in range(chunks):
-        here = pl.ds(c * width, width)
-        acc[...] = jnp.zeros_like(acc)
+    for c in range(chunks):
+        here = pl.ds(c * width, width)
+        under[here] = jnp.zeros((width, K, L), jnp.float32)
         for d in range(1, ny):
             @pl.when(my >= d)
             def _(d=d, c=c, here=here):
                 total_copy(d, c).wait_recv()
-                acc[...] = acc[...] + below[d - 1, here]
-
-        def running(q, carry, c=c):
-            i = c * width + q
-            value = acc[q]
-            for j in range(J):
-                value = value + u[STEPS % 2, j + 1, i + 1]
-                csum[j, i] = value * scale
-            return carry
-
-        lax.fori_loop(0, width, running, 0)
-        sum_copy(c).start()
+                under[here] = under[here] + below[d - 1, here]
 
     for side in (0, 1):
         for c in range(chunks):
@@ -231,10 +207,36 @@
             @pl.when(my + d < ny)
             def _(d=d, c=c):
                 total_copy(d, c).wait_send()
-        for part in (1, 2):
-            out_copy(part, c).wait()
+
+
+def sums_kernel(scale, chunks, end, under, sums_out, field_out, csum, sum_sem, out_sem):
+    J, I = end.shape[:2]
+    width = I // chunks
+
+    def out_copy(c):
+        here = pl.ds(c * width, width)
+        return pltpu.make_async_copy(end.at[:, here], field_out.at[:, here], out_sem.at[c])
+
+    def sum_copy(c):
+        here = pl.ds(c * width, width)
+        return pltpu.make_async_copy(csum.at[:, here], sums_out.at[:, here], sum_sem.at[c])
+
+    for c in range(chunks):
+        out_copy(c).start()
+    for c in range(chunks):
+        def running(q, carry, c=c):
+            i = c * width + q
+            value = under[i]
+            for j in range(J):
+                value = value + end[j, i]
+                csum[j, i] = value * scale
+            return carry
+
+        lax.fori_loop(0, width, running, 0)
+        sum_copy(c).start()
+    for c in range(chunks):
+        out_copy(c).wait()
         sum_copy(c).wait()
-    out_copy(0, 0).wait()
 
 
 def local(peers, field_now, earlier, speed_square):
@@ -246,21 +248,20 @@
     anywhere = pl.BlockSpec(memory_space=pltpu.MemorySpace.HBM)
     shape = jax.ShapeDtypeStruct(field_now.shape, f32)
     slots = max(ny - 1, 1)
-    return pl.pallas_call(
+    resident = pl.BlockSpec(memory_space=pltpu.VMEM)
+    end, under = pl.pallas_call(
         functools.partial(march_kernel, peers, chunks),
-        out_shape=(shape, shape),
+        out_shape=(pltpu.VMEM((J, I, K, L), f32), pltpu.VMEM((I, K, L), f32)),
         in_specs=[anywhere] * 3,
-        out_specs=(anywhere, anywhere),
+        out_specs=(resident, resident),
         scratch_shapes=[
             pltpu.VMEM((2, J + 2, I + 2, K, L), f32),
             pltpu.VMEM((J, I, K, L), f32),
-            pltpu.VMEM((J, I, K, L), f32),
             pltpu.VMEM((I, K, L), f32),
-            pltpu.VMEM((I // chunks, K, L), f32),
             pltpu.VMEM((slots, I, K, L), f32),
             pltpu.VMEM((STEPS, 2, J, I, L), f32),
             pltpu.VMEM((STEPS, 2, J, I, L), f32),
-            dma((3,)),
+            dma((5,)),
             dma((STEPS, 2, chunks)),
             dma((STEPS, 2, chunks)),
             dma((STEPS, 2, 3)),
@@ -269,14 +270,21 @@
             dma((STEPS, 2, 3)),
             dma((slots, chunks)),
             dma((slots, chunks)),
-            dma((3, chunks)),
-            dma((chunks,)),
         ],
         compiler_params=pltpu.CompilerParams(
-            collective_id=0, has_side_effects=True, vmem_limit_bytes=60 * 1024 * 1024
+            collective_id=0, has_side_effects=True, vmem_limit_bytes=55 * 1024 * 1024
         ),
         name="march",
     )(field_now, earlier, speed_square)
+    return pl.pallas_call(
+        functools.partial(sums_kernel, 1.0 / (J * ny), chunks),
+        out_shape=(shape, shape),
+        in_specs=[resident] * 2,
+        out_specs=(anywhere, anywhere),
+        scratch_shapes=[pltpu.VMEM((J, I, K, L), f32), dma((chunks,)), dma((chunks,))],
+        compiler_params=pltpu.CompilerParams(vmem_limit_bytes=16 * 1024 * 1024),
+        name="sums",
+    )(end, under)
 
 
 def solution(mesh):

time: 116 us -> 112 us (0.966)
  local copies, waits for them, and re-layouts: 6.96 us -> 0 us
  Pallas kernels: 108 us -> 111 us
    unnamed x4 -> x0, local copies, waits for them, and re-layouts: 6.96 us -> none
    pallas_call x0 -> x1, Pallas kernels: none -> 3.37 us  [local(): pl.pallas_call(functools.partial(sums_kernel, 1.0 / (J * ny), chunks), ou...]
where the time goes in v2:
time: 112 us
  Pallas kernels  111 us (99%)
    pallas_call x1, Pallas kernels, local(): pl.pallas_call(functools.partial(march_kernel, peers, chunks), out_shape=...  108 us
    pallas_call x1, Pallas kernels, local(): pl.pallas_call(functools.partial(sums_kernel, 1.0 / (J * ny), chunks), ou...  3.37 us

profile of v2, /device:TPU:0, one launch (start us, length us, event | category | flops | bytes accessed | tf_op | source)
XLA Modules:
  0.0 111.8 jit_solution(17000789711229428142)
XLA Ops:
  0.6 107.7 %march.1 = (f32[8,16,64,128]{3,2,1,0:T(8,128)S(1)}, f32[16,64,128]{2,1,0:T(8,128)S(1)}) custom-call(f32[8,16,64,128]{3,2,1,0:T(8,128)} %field.1, f32[8,16,64,128]{3,2,1,0:T(8,128)} %before.1, f32[8,16,64,128]{3,2,1,0:T(8,128)} %speed.1), custom_call_target="tpu_custom_call" | custom-call | tf_op jit(solution)/shard_map/march/pallas_call | solution.py:252
  108.4 3.4 %sums.1 = (f32[8,16,64,128]{3,2,1,0:T(8,128)}, f32[8,16,64,128]{3,2,1,0:T(8,128)}) custom-call(f32[8,16,64,128]{3,2,1,0:T(8,128)S(1)} %get-tuple-element.4.end, f32[16,64,128]{2,1,0:T(8,128)S(1)} %get-tuple-element.5.under), custom_call_target="tpu_custom_call" | custom-call | tf_op jit(solution)/shard_map/sums/pallas_call | solution.py:279

commit v3 on v2

--- a/solution.py
+++ b/solution.py
@@ -15,7 +15,7 @@
 def march_kernel(
     peers, chunks, field, before, speed, end, under,
     u, cs, total, below, ysend, yrecv,
-    load_sem, x_send, x_recv, z_send, z_recv, y_send, y_recv, t_send, t_recv,
+    load_sem, x_send, x_recv, z_send, z_recv, y_send, y_recv, t_send, t_recv, word,
 ):
     J, I, K, L = field.shape
     ny, nx, nz = peers
@@ -35,15 +35,38 @@
         pltpu.make_async_copy(before, u.at[1, pl.ds(1, J), pl.ds(1, I)], load_sem.at[3]),
         pltpu.make_async_copy(speed, cs, load_sem.at[4]),
     ]
+    barrier = pltpu.get_barrier_semaphore()
+    above, under_me = mx < nx - 1, mx > 0
+
+    def greet(to):
+        pl.semaphore_signal(barrier, inc=1, device_id=to, device_id_type=MESH)
+
+    for d in range(1, ny):
+        greet({"py": lax.rem(my + d, ny)})
+    for side in z_side:
+        greet(side)
+
+    @pl.when(above)
+    def _():
+        greet(x_side[0])
+
+    @pl.when(under_me)
+    def _():
+        greet(x_side[1])
+
     for load in loads:
         load.start()
-
-    barrier = pltpu.get_barrier_semaphore()
-    for d in range(1, ny):
-        pl.semaphore_signal(barrier, inc=1, device_id={"py": lax.rem(my + d, ny)}, device_id_type=MESH)
-    for side in x_side + z_side:
-        pl.semaphore_signal(barrier, inc=1, device_id=side, device_id_type=MESH)
-    pl.semaphore_wait(barrier, ny - 1 + 4)
+    pl.semaphore_wait(barrier, ny - 1 + 2 + jnp.where(above, 1, 0) + jnp.where(under_me, 1, 0))
+
+    def hand_on():
+        for way, (comes, goes) in enumerate(((under_me, above), (above, under_me))):
+            @pl.when(comes)
+            def _(way=way):
+                pl.semaphore_wait(word.at[way], 1)
+
+            @pl.when(goes)
+            def _(way=way):
+                pl.semaphore_signal(word.at[way], inc=1, device_id=x_side[way], device_id_type=MESH)
 
     def remote(src, dst, send, recv, to):
         return pltpu.make_async_remote_copy(
@@ -79,6 +102,7 @@
     for c in range(chunks):
         for side in (0, 1):
             j_copy(0, side, c).start()
+    hand_on()
     for part in range(3):
         for side in (0, 1):
             i_copy(0, side, part).start()
@@ -270,6 +294,7 @@
             dma((STEPS, 2, 3)),
             dma((slots, chunks)),
             dma((slots, chunks)),
+            pltpu.SemaphoreType.REGULAR((2,)),
         ],
         compiler_params=pltpu.CompilerParams(
             collective_id=0, has_side_effects=True, vmem_limit_bytes=55 * 1024 * 1024

time: 112 us -> 110 us (0.982)
    pallas_call x1, Pallas kernels: 108 us -> 106 us  [local(): pl.pallas_call(functools.partial(march_kernel, peers, chunks), out_shape=...]
where the time goes in v3:
time: 110 us
  Pallas kernels  110 us (100%)
    pallas_call x1, Pallas kernels, local(): pl.pallas_call(functools.partial(march_kernel, peers, chunks), out_shape=...  106 us
    pallas_call x1, Pallas kernels, local(): pl.pallas_call(functools.partial(sums_kernel, 1.0 / (J * ny), chunks), ou...  3.37 us

profile of v3, /device:TPU:0, one launch (start us, length us, event | category | flops | bytes accessed | tf_op | source)
XLA Modules:
  0.0 110.3 jit_solution(5139085503208146521)
XLA Ops:
  0.6 106.2 %march.1 = (f32[8,16,64,128]{3,2,1,0:T(8,128)S(1)}, f32[16,64,128]{2,1,0:T(8,128)S(1)}) custom-call(f32[8,16,64,128]{3,2,1,0:T(8,128)} %field.1, f32[8,16,64,128]{3,2,1,0:T(8,128)} %before.1, f32[8,16,64,128]{3,2,1,0:T(8,128)} %speed.1), custom_call_target="tpu_custom_call" | custom-call | tf_op jit(solution)/shard_map/march/pallas_call | solution.py:276
  106.9 3.4 %sums.1 = (f32[8,16,64,128]{3,2,1,0:T(8,128)}, f32[8,16,64,128]{3,2,1,0:T(8,128)}) custom-call(f32[8,16,64,128]{3,2,1,0:T(8,128)S(1)} %get-tuple-element.4.end, f32[16,64,128]{2,1,0:T(8,128)S(1)} %get-tuple-element.5.under), custom_call_target="tpu_custom_call" | custom-call | tf_op jit(solution)/shard_map/sums/pallas_call | solution.py:304

commit v4 on v3

--- a/solution.py
+++ b/solution.py
@@ -54,7 +54,7 @@
     def _():
         greet(x_side[1])
 
-    for load in loads:
+    for load in loads[:2]:
         load.start()
     pl.semaphore_wait(barrier, ny - 1 + 2 + jnp.where(above, 1, 0) + jnp.where(under_me, 1, 0))
 
@@ -102,6 +102,8 @@
     for c in range(chunks):
         for side in (0, 1):
             j_copy(0, side, c).start()
+    for load in loads[2:]:
+        load.start()
     hand_on()
     for part in range(3):
         for side in (0, 1):

time: 110 us -> 110 us (level)
  no operation moved by 1% of the time
where the time goes in v4:
time: 110 us
  Pallas kernels  110 us (100%)
    pallas_call x1, Pallas kernels, local(): pl.pallas_call(functools.partial(march_kernel, peers, chunks), out_shape=...  106 us
    pallas_call x1, Pallas kernels, local(): pl.pallas_call(functools.partial(sums_kernel, 1.0 / (J * ny), chunks), ou...  3.37 us

profile of v4, /device:TPU:0, one launch (start us, length us, event | category | flops | bytes accessed | tf_op | source)
XLA Modules:
  0.0 110.3 jit_solution(14398247628325664768)
XLA Ops:
  0.6 106.2 %march.1 = (f32[8,16,64,128]{3,2,1,0:T(8,128)S(1)}, f32[16,64,128]{2,1,0:T(8,128)S(1)}) custom-call(f32[8,16,64,128]{3,2,1,0:T(8,128)} %field.1, f32[8,16,64,128]{3,2,1,0:T(8,128)} %before.1, f32[8,16,64,128]{3,2,1,0:T(8,128)} %speed.1), custom_call_target="tpu_custom_call" | custom-call | tf_op jit(solution)/shard_map/march/pallas_call | solution.py:278
  106.9 3.4 %sums.1 = (f32[8,16,64,128]{3,2,1,0:T(8,128)}, f32[8,16,64,128]{3,2,1,0:T(8,128)}) custom-call(f32[8,16,64,128]{3,2,1,0:T(8,128)S(1)} %get-tuple-element.4.end, f32[16,64,128]{2,1,0:T(8,128)S(1)} %get-tuple-element.5.under), custom_call_target="tpu_custom_call" | custom-call | tf_op jit(solution)/shard_map/sums/pallas_call | solution.py:306
